TPU v7x, 32 devices: a whole 2x2x4 slice. The times are simulated.
32 devices in a mesh: lat: 4 (over y, x), lon: 8 (over z, core).
Axes of the slice: x: 2, y: 2, z: 4, core: 2. Of those that a mesh axis runs over, the one named last changes fastest.
Arguments:
- pressure: float32 [4, 30, 5120], P('lat', None, 'lon'), may hold values from -6 to 6
- velocity: float32 [4, 30, 7680], P('lat', None, 'lon'), may hold values from -6 to 6
- edge_cells: int32 [4, 2, 7680], P('lat', None, 'lon'), may hold values from 0 to 1663
- cell_edges: int32 [4, 3, 5120], P('lat', None, 'lon'), may hold values from 0 to 1983
- send_cells: int32 [4, 8, 1024], P('lat', None, 'lon'), may hold values from 0 to 639
- send_edges: int32 [4, 8, 1024], P('lat', None, 'lon'), may hold values from 0 to 959
- inv_dual: float32 [4, 7680], P('lat', 'lon'), may hold values from 0.5 to 2
- edge_weight: float32 [4, 3, 5120], P('lat', None, 'lon'), may hold values from -3 to 3
- sound_speed: float32 [4, 5120], P('lat', 'lon'), may hold values from 0.1 to 0.6
- coupling: float32 [4, 30, 5120], P('lat', None, 'lon'), may hold values from 0.1 to 2
Outputs:
- pressure_out: float32 [4, 30, 5120], P('lat', None, 'lon')
- velocity_out: float32 [4, 30, 7680], P('lat', None, 'lon')
Inputs may be any that keep to these rules, and one draw needn't show every extreme that they name: `edge_cells`: positions below 640 are own cells; position 640 + r * 128 + j is slot j of the halo piece from the neighbour at offset number r. `cell_edges`: positions below 960 are own edges; position 960 + r * 128 + j is slot j of the edge halo piece from the neighbour at offset number r. `send_cells`: indices of own cells. `send_edges`: indices of own edges.
All inputs are finite; a program needn't handle non-finite values.
Results may differ from a plain program's by a relative error of at most 0.0001.
Values sent between devices are 32-bit elements; how exact they have to be, the bound alone decides.
A program may use at most 64 MiB of HBM per device.

v0:
```python
import jax
import jax.numpy as jnp
from jax import lax
from jax.experimental import pallas as pl
from jax.experimental.pallas import tpu as pltpu
from jax.sharding import PartitionSpec as P

NSUB = 3
OFFSETS = ((-1, -1), (-1, 0), (-1, 1), (0, -1), (0, 1), (1, -1), (1, 0), (1, 1))
LANES = 128
step_scale = 0.5
MESH = pl.DeviceIdType.MESH
F32 = jnp.float32


def round_up(n, m):
    return (n + m - 1) // m * m


def tiles_of(ref, width):
    return [ref[:, k * LANES : (k + 1) * LANES] for k in range(width // LANES)]


def spread(index, own, padded):
    return jnp.where(index >= own, index + (padded - own), index)


def member_of(p, q):
    return (1 + q, 3 + (q + 1) // 2, 6 + q)[p + 1]


def kernel(
    n_lat, n_lon, nlev, cells, edges, halo,
    p_hbm, v_hbm, ec_hbm, ce_hbm, sc_hbm, se_hbm, inv_hbm, weight_hbm, sound_hbm, coupling_hbm,
    p_out, v_out,
    p_row, v_row, ec, ce, sc, se, inv_dual, weight, sound, coupling,
    pf, vf, p_send, v_send, p_halo, v_halo,
    t_inv, t_low, t_up, work, grad, div,
    p_ss, p_rs, v_ss, v_rs, in_sem,
):
    a, b = lax.axis_index("lat"), lax.axis_index("lon")
    ccols, ecols = pf.shape[1], vf.shape[1]
    below, above = a > 0, a < n_lat - 1
    far = 2 * ((2 * b) // n_lon) - 1
    near = -far
    sends = [(-1, far), (1, far), (0, far), (-1, 0), (1, 0), (-1, near), (1, near), (0, near)]
    arrivals = [[(0, near), (-1, 0), (1, 0), (-1, near), (1, near), (0, far)], [(-1, far), (1, far)]]

    def if_there(p, fn):
        if p == 0:
            fn()
        else:
            pl.when(below if p < 0 else above)(fn)

    def target(p, q):
        return (a + p, lax.rem(b + q + n_lon, n_lon))

    barrier = pltpu.get_barrier_semaphore()
    for lat_step in (-1, 1, 0):
        def greet(lat_step=lat_step):
            for offset in OFFSETS:
                if offset[0] == lat_step:
                    pl.semaphore_signal(
                        barrier, inc=1, device_id=target(*offset), device_id_type=MESH
                    )
        if_there(lat_step, greet)

    pairs = [
        (coupling_hbm, coupling), (p_hbm, p_row), (sc_hbm, sc), (ec_hbm, ec), (v_hbm, v_row),
        (inv_hbm, inv_dual), (se_hbm, se), (ce_hbm, ce), (weight_hbm, weight), (sound_hbm, sound),
    ]
    loads = [pltpu.make_async_copy(x, y, in_sem.at[k]) for k, (x, y) in enumerate(pairs)]
    for load in loads:
        load.start()

    def clear(p):
        def fill():
            for slot, offset in enumerate(OFFSETS):
                if offset[0] == p:
                    p_halo[slot] = jnp.zeros(p_halo.shape[1:], F32)
                    v_halo[slot] = jnp.zeros(v_halo.shape[1:], F32)
        return fill

    pl.when(a == 0)(clear(-1))
    pl.when(a == n_lat - 1)(clear(1))
    pf[nlev - nlev % 8 :, :] = jnp.zeros_like(pf[nlev - nlev % 8 :, :])
    vf[...] = jnp.zeros_like(vf)

    def copy(p, q, send, land, ss, rs):
        member = member_of(p, q)
        return pltpu.make_async_remote_copy(
            src_ref=send.at[member], dst_ref=land.at[7 - member],
            send_sem=ss.at[member], recv_sem=rs.at[7 - member],
            device_id=target(p, q), device_id_type=MESH,
        )

    def collect(tiles, lists, send, offsets):
        for p, q in offsets:
            index = lists[0, pl.ds(member_of(p, q), 1), :]
            send[member_of(p, q)] = pick(tiles, range(len(tiles)), index)

    def launch(offsets, *refs):
        for p, q in offsets:
            if_there(p, lambda: copy(p, q, *refs).start())

    def arrive(group, *refs):
        for p, q in group:
            if_there(p, lambda: copy(-p, -q, *refs).wait_recv())

    def retire(*refs):
        for p, q in sends:
            if_there(p, lambda: copy(p, q, *refs).wait_send())

    def pick(tiles, firsts, index):
        shape = tiles[0].shape
        lane = jnp.broadcast_to(index & (LANES - 1), shape)
        tile = jnp.broadcast_to(index >> 7, shape)
        out = jnp.zeros(shape, F32)
        for values, first in zip(tiles, firsts):
            moved = jnp.take_along_axis(values, lane, axis=1, mode="promise_in_bounds")
            out = jnp.where(tile == first, moved, out)
        return out

    def halo_tiles(land, group, own):
        slots = [member_of(p, q) for p, q in group]
        return [land[slot] for slot in slots], [own + slot for slot in slots]

    def edge_columns(ref, row, k):
        stop = min(edges, (k + 1) * LANES)
        part = row(ref)[:, k * LANES : stop]
        short = (k + 1) * LANES - stop
        return jnp.pad(part, ((0, 0), (0, short))) if short else part

    def add_gradient(tiles, firsts, fresh, last):
        for k in range(ecols // LANES):
            cols = slice(k * LANES, (k + 1) * LANES)
            taken = [
                pick(tiles, firsts, spread(edge_columns(ec, lambda ref: ref[0, r : r + 1, :], k), cells, ccols))
                for r in (0, 1)
            ]
            change = taken[1] - taken[0]
            total = change if fresh else grad[:, cols] + change
            if last:
                scale = step_scale * edge_columns(inv_dual, lambda ref: ref[...], k)
                vf[:, cols] = vf[:, cols] - scale * total
            else:
                grad[:, cols] = total

    def add_divergence(tiles, firsts, fresh, last):
        for k in range(ccols // LANES):
            cols = slice(k * LANES, (k + 1) * LANES)
            total = None if fresh else div[:, cols]
            for j in range(3):
                term = pick(tiles, firsts, spread(ce[j, :, cols], edges, ecols)) * weight[j, :, cols]
                total = term if total is None else total + term
            if last:
                right = pf[:, cols] - sound[:, cols] * total
                work[0:nlev, cols] = right[0:nlev] * t_inv[:, cols]
            else:
                div[:, cols] = total

    def columns_solved():
        ratio = None
        for level in range(nlev):
            here = coupling[level]
            if level == 0:
                divisor = 1.0 + here
            else:
                lower = coupling[level - 1]
                divisor = 1.0 + lower + here + lower * ratio
            inverse = 1.0 / divisor
            ratio = -here * inverse
            t_inv[level : level + 1, :] = inverse
            t_up[level : level + 1, :] = ratio
            if level > 0:
                t_low[level : level + 1, :] = lower * inverse

    p_refs = (p_send, p_halo, p_ss, p_rs)
    v_refs = (v_send, v_halo, v_ss, v_rs)
    for load in loads[:3]:
        load.wait()
    for level in range(nlev):
        pf[level : level + 1, :] = p_row[level]
    own = tiles_of(pf, ccols)
    collect(own, sc, p_send, sends)
    columns_solved()
    bands = (a + n_lat - 1) // n_lat + (2 * n_lat - 2 - a) // n_lat
    pl.semaphore_wait(barrier, 2 + 3 * bands)

    for substep in range(NSUB):
        final = substep == NSUB - 1
        if substep == 0:
            launch(sends, *p_refs)
            for load in loads[3:]:
                load.wait()
            for level in range(nlev):
                vf[level : level + 1, 0:edges] = v_row[level]
        else:
            own = tiles_of(pf, ccols)
            for part in (sends[:3], sends[3:]):
                collect(own, sc, p_send, part)
                launch(part, *p_refs)
        add_gradient(own, range(len(own)), True, False)
        if substep > 0:
            retire(*v_refs)
        for k, group in enumerate(arrivals):
            arrive(group, *p_refs)
            add_gradient(*halo_tiles(p_halo, group, ccols // LANES), False, k == 1)

        own = tiles_of(vf, ecols)
        for part in (sends[:3], sends[3:]):
            collect(own, se, v_send, part)
            launch(part, *v_refs)
        if final:
            for level in range(nlev):
                v_out[level] = vf[level : level + 1, 0:edges]
        add_divergence(own, range(len(own)), True, False)
        retire(*p_refs)
        for k, group in enumerate(arrivals):
            arrive(group, *v_refs)
            add_divergence(*halo_tiles(v_halo, group, ecols // LANES), False, k == 1)

        current = work[0:1, :]
        for level in range(1, nlev):
            current = work[level : level + 1, :] + t_low[level : level + 1, :] * current
            work[level : level + 1, :] = current
        for level in range(nlev - 1, -1, -1):
            if level < nlev - 1:
                current = work[level : level + 1, :] - t_up[level : level + 1, :] * current
            if final:
                p_out[level] = current
            else:
                pf[level : level + 1, :] = current

    retire(*v_refs)


def write_out(p_ref, v_ref, p_out, v_out, sem):
    stores = [
        pltpu.make_async_copy(x, y, sem.at[k])
        for k, (x, y) in enumerate(((v_ref, v_out), (p_ref, p_out)))
    ]
    for store in stores:
        store.start()
    for store in stores:
        store.wait()


def level_major(x):
    return jnp.transpose(x, (1, 0, 2))


def on_device(*args):
    pressure, velocity, send_cells = args[0], args[1], args[4]
    n_lat, n_lon = lax.axis_size("lat"), lax.axis_size("lon")
    nlev, cells, edges = pressure.shape[1], pressure.shape[2], velocity.shape[2]
    halo = send_cells.shape[2]
    rows, ecols = round_up(nlev, 32), round_up(edges, 128)
    hbm = pl.BlockSpec(memory_space=pltpu.HBM)
    vmem = pl.BlockSpec(memory_space=pltpu.VMEM)
    dma8 = pltpu.SemaphoreType.DMA((8,))
    args = [level_major(x) if k in (0, 1, 3, 7, 9) else x for k, x in enumerate(args)]

    def body(*refs):
        kernel(n_lat, n_lon, nlev, cells, edges, halo, *refs)

    halo_shape = pltpu.VMEM((8, rows, halo), F32)
    cell_shape = pltpu.VMEM((rows, cells), F32)
    edge_shape = pltpu.VMEM((rows, ecols), F32)
    level_shape = pltpu.VMEM((nlev, cells), F32)
    outs = pl.pallas_call(
        body,
        name="substeps",
        out_shape=(
            pltpu.VMEM(args[0].shape, F32),
            pltpu.VMEM(args[1].shape, F32),
        ),
        in_specs=[hbm] * len(args),
        out_specs=(vmem, vmem),
        scratch_shapes=[pltpu.VMEM(x.shape, x.dtype) for x in args] + [
            cell_shape, edge_shape, halo_shape, halo_shape, halo_shape, halo_shape,
            level_shape, level_shape, level_shape, cell_shape, edge_shape, cell_shape,
            dma8, dma8, dma8, dma8,
            pltpu.SemaphoreType.DMA((len(args),)),
        ],
        compiler_params=pltpu.CompilerParams(
            collective_id=0, has_side_effects=True, vmem_limit_bytes=66_000_000
        ),
    )(*args)
    outs = pl.pallas_call(
        write_out,
        name="write_out",
        out_shape=tuple(jax.ShapeDtypeStruct(x.shape, F32) for x in outs),
        in_specs=[vmem] * 2,
        out_specs=(hbm, hbm),
        scratch_shapes=[pltpu.SemaphoreType.DMA((2,))],
        compiler_params=pltpu.CompilerParams(vmem_limit_bytes=1024 * 1024),
    )(*outs)
    return tuple(level_major(x) for x in outs)


def solution(mesh):
    band = P("lat", None, "lon")
    flat = P("lat", "lon")
    return jax.shard_map(
        on_device,
        mesh=mesh,
        in_specs=(band, band, band, band, band, band, flat, band, flat, band),
        out_specs=(band, band),
        check_vma=False,
    )
```

profile of v0, /device:TPU:0, one launch (start us, length us, event | category | flops | bytes accessed | tf_op | source)
XLA Modules:
  0.0 35.3 jit_solution(40665829855898827)
XLA Ops:
  0.6 33.9 %substeps.1 = (f32[30,1,640]{2,1,0:T(1,128)S(1)}, f32[30,1,960]{2,1,0:T(1,128)S(1)}) custom-call(f32[30,1,640]{2,1,0:T(1,128)} %bitcast.8, f32[30,1,960]{2,1,0:T(1,128)} %bitcast.7, s32[1,2,960]{2,1,0:T(2,128)} %refs_2_.1, s32[3,1,640]{2,1,0:T(1,128)} %bitcast.10, s32[1,8,128]{2,1,0:T(8,128)} %refs_4_.1, s32[1,8,128]{2,1,0:T(8,128)} %refs_5_.1, ...), custom_call_target="tpu_custom_call" | custom-call | tf_op jit(solution)/shard_map/substeps/pallas_call | solution.py:271
  34.6 0.7 %write_out.1 = (f32[30,1,640]{2,1,0:T(1,128)}, f32[30,1,960]{2,1,0:T(1,128)}) custom-call(f32[30,1,640]{2,1,0:T(1,128)S(1)} %get-tuple-element.6.p_ref, f32[30,1,960]{2,1,0:T(1,128)S(1)} %get-tuple-element.7.v_ref), custom_call_target="tpu_custom_call" | custom-call | tf_op jit(solution)/shard_map/write_out/pallas_call | solution.py:290
where the time goes:
time: 35.4 us; the launch traced here: 35.3 us
  Pallas kernels  34.6 us (98%)
  between operations  0.64 us (2%)
    pallas_call x1, Pallas kernels, on_device(): pl.pallas_call(body, name='substeps', out_shape=(pltpu.VMEM(args[0].shape...  33.9 us

commit v1 on v0

v1 whole, which is shorter than its diff:
```python
import math

import jax
import jax.numpy as jnp
from jax import lax
from jax.experimental import pallas as pl
from jax.experimental.pallas import tpu as pltpu
from jax.sharding import PartitionSpec as P

NSUB = 3
OFFSETS = ((-1, -1), (-1, 0), (-1, 1), (0, -1), (0, 1), (1, -1), (1, 0), (1, 1))
LANES = 128
step_scale = 0.5
MESH = pl.DeviceIdType.MESH
F32 = jnp.float32


def round_up(n, m):
    return (n + m - 1) // m * m


def tiles_of(ref, width):
    return [ref[:, k * LANES : (k + 1) * LANES] for k in range(width // LANES)]


def spread(index, own, padded):
    return jnp.where(index >= own, index + (padded - own), index)


def member_of(p, q):
    if isinstance(p, int) and p == 0:
        return 3 + (q + 1) // 2
    return (7 + 5 * p) // 2 + q


def kernel(
    n_lat, n_lon, nlev, cells, edges, halo,
    p_hbm, v_hbm, ec_hbm, ce_hbm, sc_hbm, se_hbm, inv_hbm, weight_hbm, sound_hbm, coupling_hbm,
    p_out, v_out,
    p_row, v_row, ec, ce, sc, se, inv_dual, weight, sound, coupling,
    pf, vf, p_send, v_send, p_halo, v_halo,
    t_inv, t_low, t_up, t_mid, work, grad, div,
    sc_list, se_list, ec_list, ce_list, scale_list, weight_list, sound_list,
    s_inv, s_low, s_up, s_mid, s_grad, s_div,
    p_ss, p_rs, v_ss, v_rs, in_sem,
):
    a, b = lax.axis_index("lat"), lax.axis_index("lon")
    ccols, ecols = pf.shape[1], vf.shape[1]
    rows = pf.shape[0]
    pieces = len(OFFSETS)
    middle = nlev // 2
    side = math.isqrt(n_lat)
    slow = jnp.where(lax.rem(a, side) == side - 1, 1, -1)
    quick = -slow
    far = 2 * lax.rem(b, 2) - 1
    near = -far
    sends = [
        (slow, far), (slow, near), (slow, 0), (quick, far), (0, far),
        (quick, near), (quick, 0), (0, near),
    ]
    p_batches = (range(0, 1), range(1, 5), range(5, 8),)
    v_batches = (range(0, 1), range(1, 3), range(3, 5), range(5, 8),)

    def if_there(p, fn):
        if isinstance(p, int) and p == 0:
            fn()
        else:
            pl.when((a + p >= 0) & (a + p < n_lat))(fn)

    def target(p, q):
        return (a + p, lax.rem(b + q + n_lon, n_lon))

    barrier = pltpu.get_barrier_semaphore()
    for lat_step in (-1, 1, 0):
        def greet(lat_step=lat_step):
            for offset in OFFSETS:
                if offset[0] == lat_step:
                    pl.semaphore_signal(
                        barrier, inc=1, device_id=target(*offset), device_id_type=MESH
                    )
        if_there(lat_step, greet)

    pairs = [
        (p_hbm, p_row), (sc_hbm, sc), (ec_hbm, ec), (v_hbm, v_row), (se_hbm, se),
        (inv_hbm, inv_dual), (coupling_hbm, coupling), (ce_hbm, ce), (weight_hbm, weight), (sound_hbm, sound),
    ]
    loads = [pltpu.make_async_copy(x, y, in_sem.at[k]) for k, (x, y) in enumerate(pairs)]
    for load in loads:
        load.start()

    def clear(p):
        def fill():
            for slot, offset in enumerate(OFFSETS):
                if offset[0] == p:
                    for turn in range(2):
                        p_halo[turn, slot] = jnp.zeros(p_halo.shape[2:], F32)
                        v_halo[turn, slot] = jnp.zeros(v_halo.shape[2:], F32)
        return fill

    pl.when(a == 0)(clear(-1))
    pl.when(a == n_lat - 1)(clear(1))
    pf[nlev - nlev % 8 :, :] = jnp.zeros_like(pf[nlev - nlev % 8 :, :])
    work[nlev - nlev % 8 :, :] = jnp.zeros_like(pf[nlev - nlev % 8 :, :])
    vf[...] = jnp.zeros_like(vf)

    def copy(i, send, land, ss, rs, turn):
        p, q = sends[i]
        member = member_of(p, q)
        return pltpu.make_async_remote_copy(
            src_ref=send.at[pl.ds(i * rows, rows)], dst_ref=land.at[turn, 7 - member],
            send_sem=ss.at[i], recv_sem=rs.at[7 - member],
            device_id=target(p, q), device_id_type=MESH,
        )

    def launch(batch, refs, turn):
        for i in batch:
            if_there(sends[i][0], lambda: copy(i, *refs, turn).start())

    def arrive(group, refs, turn):
        send, land, ss, rs = refs
        for p, q in group:
            slot = member_of(p, q)

            def wait():
                pltpu.make_async_remote_copy(
                    src_ref=send.at[pl.ds(0, rows)], dst_ref=land.at[turn, slot],
                    send_sem=ss.at[0], recv_sem=rs.at[slot],
                    device_id=target(p, q), device_id_type=MESH,
                ).wait_recv()
            if_there(p, wait)

    def retire(refs, turn):
        for i in range(pieces):
            if_there(sends[i][0], lambda: copy(i, *refs, turn).wait_send())

    def pick(tiles, firsts, index):
        shape = tiles[0].shape
        lane = jnp.broadcast_to(index & (LANES - 1), shape)
        tile = jnp.broadcast_to(index >> 7, shape)
        out = jnp.zeros(shape, tiles[0].dtype)
        for values, first in zip(tiles, firsts):
            moved = jnp.take_along_axis(values, lane, axis=1, mode="promise_in_bounds")
            out = jnp.where(tile == first, moved, out)
        return out

    def own_part(tiles):
        return tiles, range(len(tiles))

    def halo_part(land, turn, group, own):
        slots = [member_of(p, q) for p, q in group]
        return [land[turn, slot] for slot in slots], [own + slot for slot in slots]

    def edge_columns(ref, row, k):
        stop = min(edges, (k + 1) * LANES)
        part = row(ref)[:, k * LANES : stop]
        short = (k + 1) * LANES - stop
        return jnp.pad(part, ((0, 0), (0, short))) if short else part

    def span(i):
        return slice(i * rows, (i + 1) * rows)

    def listed(row_tiles, index):
        shape = (pieces, LANES)
        tiles = [jnp.broadcast_to(tile, shape) for tile in row_tiles]
        return pick(tiles, range(len(tiles)), index)

    def piece_change(i, part):
        low, high = (pick(*part, ec_list[r, i : i + 1, :]) for r in (0, 1))
        return high - low

    def piece_sum(i, part):
        total = None
        for j in range(3):
            term = pick(*part, ce_list[j, i : i + 1, :]) * weight_list[j, i : i + 1, :]
            total = term if total is None else total + term
        return total

    def add_gradient(part, fresh, last):
        for k in range(ecols // LANES):
            cols = slice(k * LANES, (k + 1) * LANES)
            taken = [
                pick(*part, spread(edge_columns(ec, lambda ref: ref[0, r : r + 1, :], k), cells, ccols))
                for r in (0, 1)
            ]
            change = taken[1] - taken[0]
            total = change if fresh else grad[:, cols] + change
            if last:
                scale = step_scale * edge_columns(inv_dual, lambda ref: ref[...], k)
                vf[:, cols] = vf[:, cols] - scale * total
            else:
                grad[:, cols] = total

    def add_divergence(part, fresh, last):
        for k in range(ccols // LANES):
            cols = slice(k * LANES, (k + 1) * LANES)
            total = None if fresh else div[:, cols]
            for j in range(3):
                term = pick(*part, spread(ce[j, :, cols], edges, ecols)) * weight[j, :, cols]
                total = term if total is None else total + term
            if last:
                right = pf[:, cols] - sound[:, cols] * total
                work[0:nlev, cols] = right[0:nlev] * t_inv[:, cols]
            else:
                div[:, cols] = total

    def eliminate(couple, put):
        ups = {}
        for k in [*range(middle), *range(nlev - 1, middle - 1, -1)]:
            here, below_it = couple(k), couple(k - 1) if k else None
            diagonal = 1.0 + here if k == 0 else 1.0 + below_it + here
            toward, away = (here, below_it) if k < middle else (below_it, here)
            last = ups.get(k - 1 if k < middle else k + 1)
            inverse = 1.0 / (diagonal if last is None else diagonal - away * last)
            ups[k] = toward * inverse
            put(k, inverse, None if last is None else away * inverse, ups[k])
        return 1.0 / (1.0 - ups[middle - 1] * ups[middle])

    def sweep(scaled, low, up, mid, hold, held, put):
        top = bottom = None
        for step in range(max(middle, nlev - middle)):
            k = step
            if k < middle:
                top = scaled(k) if top is None else scaled(k) + low(k) * top
                hold(k, top)
            k = nlev - 1 - step
            if k >= middle:
                bottom = scaled(k) if bottom is None else scaled(k) + low(k) * bottom
                hold(k, bottom)
        bottom = (bottom + up(middle) * top) * mid
        top = top + up(middle - 1) * bottom
        put(middle, bottom)
        put(middle - 1, top)
        for step in range(1, max(middle, nlev - middle)):
            k = middle - 1 - step
            if k >= 0:
                top = held(k) + up(k) * top
                put(k, top)
            k = middle + step
            if k < nlev:
                bottom = held(k) + up(k) * bottom
                put(k, bottom)

    def level(k):
        return slice(k, k + 1)

    def across(k, batch):
        return pl.ds(k + batch.start * rows, len(batch), stride=rows)

    def own_columns():
        def put(k, inverse, low, up):
            t_inv[level(k), :] = inverse
            t_up[level(k), :] = up
            if low is not None:
                t_low[level(k), :] = low
        t_mid[...] = eliminate(lambda k: coupling[k], put)

    def piece_columns():
        for k in range(nlev):
            work[level(k), :] = coupling[k]
        tiles = own_part(tiles_of(work, ccols))
        for i in range(pieces):
            s_div[span(i), :] = pick(*tiles, sc_list[i : i + 1, :])

        def put(k, inverse, low, up):
            s_inv[k] = inverse
            s_up[k] = up
            if low is not None:
                s_low[k] = low
        s_mid[...] = eliminate(lambda k: s_div[across(k, range(pieces)), :], put)

    def solve_pieces(batch):
        kept = {}
        some = slice(batch.start, batch.stop)

        def put(k, value):
            p_send[across(k, batch), :] = value
        sweep(
            lambda k: s_div[across(k, batch), :] * s_inv[k, some], lambda k: s_low[k, some],
            lambda k: s_up[k, some], s_mid[some, :], kept.__setitem__, kept.__getitem__, put,
        )

    def solve_own(put):
        def hold(k, value):
            work[level(k), :] = value
        sweep(
            lambda k: work[level(k), :], lambda k: t_low[level(k), :], lambda k: t_up[level(k), :], t_mid[...],
            hold, lambda k: work[level(k), :], put,
        )

    p_refs = (p_send, p_halo, p_ss, p_rs)
    v_refs = (v_send, v_halo, v_ss, v_rs)
    for load in loads[:2]:
        load.wait()
    for k in range(nlev):
        pf[level(k), :] = p_row[k]
    for i, offset in enumerate(sends):
        sc_list[i : i + 1, :] = sc[0, pl.ds(member_of(*offset), 1), :]
    own = own_part(tiles_of(pf, ccols))
    for i in range(pieces):
        p_send[span(i), :] = pick(*own, sc_list[i : i + 1, :])
    bands = (a + n_lat - 1) // n_lat + (2 * n_lat - 2 - a) // n_lat
    pl.semaphore_wait(barrier, 2 + 3 * bands)
    launch(range(pieces), p_refs, 0)

    for load in loads[2:]:
        load.wait()
    for k in range(nlev):
        vf[level(k), 0:edges] = v_row[k]
    for i, offset in enumerate(sends):
        se_list[i : i + 1, :] = se[0, pl.ds(member_of(*offset), 1), :]
    blocks = range(ecols // LANES)
    index = se_list[...]
    for r in (0, 1):
        row = [edge_columns(ec, lambda ref: ref[0, r : r + 1, :], k) for k in blocks]
        ec_list[r] = spread(listed(row, index), cells, ccols)
    scale_list[...] = step_scale * listed([edge_columns(inv_dual, lambda ref: ref[...], k) for k in blocks], index)
    own = own_part(tiles_of(vf, ecols))
    for i in range(pieces):
        v_send[span(i), :] = pick(*own, se_list[i : i + 1, :])

    def compose_cells():
        index = sc_list[...]
        cuts = [slice(k * LANES, (k + 1) * LANES) for k in range(ccols // LANES)]
        for j in range(3):
            ce_list[j] = spread(listed([ce[j, :, cut] for cut in cuts], index), edges, ecols)
            weight_list[j] = listed([weight[j, :, cut] for cut in cuts], index)
        sound_list[...] = listed([sound[:, cut] for cut in cuts], index)

    for substep in range(NSUB):
        final = substep == NSUB - 1
        turn = substep % 2
        own = own_part(tiles_of(pf, ccols))
        for i in range(pieces):
            s_grad[span(i), :] = piece_change(i, own)
        add_gradient(own, True, False)
        if substep == 0:
            compose_cells()
            piece_columns()
            own_columns()
        else:
            retire(v_refs, 1 - turn)
        arrive(sends, p_refs, turn)
        part = halo_part(p_halo, turn, sends, ccols // LANES)
        for batch in v_batches:
            for i in batch:
                change = s_grad[span(i), :] + piece_change(i, part)
                v_send[span(i), :] = v_send[span(i), :] - scale_list[i : i + 1, :] * change
            launch(batch, v_refs, turn)
        add_gradient(part, False, True)
        if final:
            for k in range(nlev):
                v_out[k] = vf[level(k), 0:edges]

        own = own_part(tiles_of(vf, ecols))
        if not final:
            for i in range(pieces):
                s_div[span(i), :] = piece_sum(i, own)
        add_divergence(own, True, False)
        retire(p_refs, turn)
        arrive(sends, v_refs, turn)
        part = halo_part(v_halo, turn, sends, ecols // LANES)
        if final:
            def put(k, value):
                p_out[k] = value
        else:
            for batch in p_batches:
                for i in batch:
                    total = s_div[span(i), :] + piece_sum(i, part)
                    s_div[span(i), :] = p_send[span(i), :] - sound_list[i : i + 1, :] * total
                solve_pieces(batch)
                launch(batch, p_refs, 1 - turn)

            def put(k, value):
                pf[level(k), :] = value
        add_divergence(part, False, True)
        solve_own(put)

    retire(v_refs, turn)


def write_out(p_ref, v_ref, p_out, v_out, sem):
    stores = [
        pltpu.make_async_copy(x, y, sem.at[k])
        for k, (x, y) in enumerate(((v_ref, v_out), (p_ref, p_out)))
    ]
    for store in stores:
        store.start()
    for store in stores:
        store.wait()


def level_major(x):
    return jnp.transpose(x, (1, 0, 2))


def on_device(*args):
    pressure, velocity, send_cells = args[0], args[1], args[4]
    n_lat, n_lon = lax.axis_size("lat"), lax.axis_size("lon")
    nlev, cells, edges = pressure.shape[1], pressure.shape[2], velocity.shape[2]
    halo = send_cells.shape[2]
    rows, ecols = round_up(nlev, 32), round_up(edges, 128)
    hbm = pl.BlockSpec(memory_space=pltpu.HBM)
    vmem = pl.BlockSpec(memory_space=pltpu.VMEM)
    dma8 = pltpu.SemaphoreType.DMA((8,))
    args = [level_major(x) if k in (0, 1, 3, 7, 9) else x for k, x in enumerate(args)]

    def body(*refs):
        kernel(n_lat, n_lon, nlev, cells, edges, halo, *refs)

    halo_shape = pltpu.VMEM((2, 8, rows, halo), F32)
    piece_shape = pltpu.VMEM((8 * rows, halo), F32)
    list_shape = pltpu.VMEM((8, halo), F32)
    places = pltpu.VMEM((8, halo), jnp.int32)
    cell_shape = pltpu.VMEM((rows, cells), F32)
    edge_shape = pltpu.VMEM((rows, ecols), F32)
    level_shape = pltpu.VMEM((nlev, cells), F32)
    stack_shape = pltpu.VMEM((nlev, 8, halo), F32)
    outs = pl.pallas_call(
        body,
        name="substeps",
        out_shape=(
            pltpu.VMEM(args[0].shape, F32),
            pltpu.VMEM(args[1].shape, F32),
        ),
        in_specs=[hbm] * len(args),
        out_specs=(vmem, vmem),
        scratch_shapes=[pltpu.VMEM(x.shape, x.dtype) for x in args] + [
            cell_shape, edge_shape, piece_shape, piece_shape, halo_shape, halo_shape,
            level_shape, level_shape, level_shape, pltpu.VMEM((1, cells), F32), cell_shape, edge_shape, cell_shape,
            places, places, pltpu.VMEM((2, 8, halo), jnp.int32), pltpu.VMEM((3, 8, halo), jnp.int32),
            list_shape, pltpu.VMEM((3, 8, halo), F32), list_shape,
            stack_shape, stack_shape, stack_shape, list_shape, piece_shape, piece_shape,
            dma8, dma8, dma8, dma8,
            pltpu.SemaphoreType.DMA((len(args),)),
        ],
        compiler_params=pltpu.CompilerParams(
            collective_id=0, has_side_effects=True, vmem_limit_bytes=66_000_000
        ),
    )(*args)
    outs = pl.pallas_call(
        write_out,
        name="write_out",
        out_shape=tuple(jax.ShapeDtypeStruct(x.shape, F32) for x in outs),
        in_specs=[vmem] * 2,
        out_specs=(hbm, hbm),
        scratch_shapes=[pltpu.SemaphoreType.DMA((2,))],
        compiler_params=pltpu.CompilerParams(vmem_limit_bytes=1024 * 1024),
    )(*outs)
    return tuple(level_major(x) for x in outs)


def solution(mesh):
    band = P("lat", None, "lon")
    flat = P("lat", "lon")
    return jax.shard_map(
        on_device,
        mesh=mesh,
        in_specs=(band, band, band, band, band, band, flat, band, flat, band),
        out_specs=(band, band),
        check_vma=False,
    )
```

time: 35.4 us -> 34.6 us (0.977)
  Pallas kernels: 34.6 us -> 33.8 us
    pallas_call x1, Pallas kernels: 33.9 us -> 33.1 us  [on_device(): pl.pallas_call(body, name='substeps', out_shape=(pltpu.VMEM(args[0].shape...]
where the time goes in v1:
time: 34.6 us; the launch traced here: 34.4 us
  Pallas kernels  33.8 us (98%)
  between operations  0.64 us (2%)
    pallas_call x1, Pallas kernels, on_device(): pl.pallas_call(body, name='substeps', out_shape=(pltpu.VMEM(args[0].shape...  33.1 us
    pallas_call x1, Pallas kernels, on_device(): pl.pallas_call(write_out, name='write_out', out_shape=tuple((jax.ShapeDty...  0.69 us

profile of v1, /device:TPU:0, one launch (start us, length us, event | category | flops | bytes accessed | tf_op | source)
XLA Modules:
  0.0 34.4 jit_solution(12068527551241622340)
XLA Ops:
  0.6 33.1 %substeps.1 = (f32[30,1,640]{2,1,0:T(1,128)S(1)}, f32[30,1,960]{2,1,0:T(1,128)S(1)}) custom-call(f32[30,1,640]{2,1,0:T(1,128)} %bitcast.8, f32[30,1,960]{2,1,0:T(1,128)} %bitcast.7, s32[1,2,960]{2,1,0:T(2,128)} %refs_2_.1, s32[3,1,640]{2,1,0:T(1,128)} %bitcast.10, s32[1,8,128]{2,1,0:T(8,128)} %refs_4_.1, s32[1,8,128]{2,1,0:T(8,128)} %refs_5_.1, ...), custom_call_target="tpu_custom_call" | custom-call | tf_op jit(solution)/shard_map/substeps/pallas_call | solution.py:418
  33.7 0.7 %write_out.1 = (f32[30,1,640]{2,1,0:T(1,128)}, f32[30,1,960]{2,1,0:T(1,128)}) custom-call(f32[30,1,640]{2,1,0:T(1,128)S(1)} %get-tuple-element.6.p_ref, f32[30,1,960]{2,1,0:T(1,128)S(1)} %get-tuple-element.7.v_ref), custom_call_target="tpu_custom_call" | custom-call | tf_op jit(solution)/shard_map/write_out/pallas_call | solution.py:440

commit v2 on v1

--- a/solution.py
+++ b/solution.py
@@ -37,14 +37,20 @@
     n_lat, n_lon, nlev, cells, edges, halo,
     p_hbm, v_hbm, ec_hbm, ce_hbm, sc_hbm, se_hbm, inv_hbm, weight_hbm, sound_hbm, coupling_hbm,
     p_out, v_out,
+    p_home, v_home, ec_home, ce_home, sc_home, se_home, inv_home, weight_home, sound_home, coupling_home,
     p_row, v_row, ec, ce, sc, se, inv_dual, weight, sound, coupling,
-    pf, vf, p_send, v_send, p_halo, v_halo,
+    pf, vf, pf_home, vf_home, h_send, p_send, v_send, p_halo, v_halo,
     t_inv, t_low, t_up, t_mid, work, grad, div,
     sc_list, se_list, ec_list, ce_list, scale_list, weight_list, sound_list,
     s_inv, s_low, s_up, s_mid, s_grad, s_div,
-    p_ss, p_rs, v_ss, v_rs, in_sem,
+    p_ss, p_rs, v_ss, v_rs, f_rs, in_sem, work_sem,
 ):
-    a, b = lax.axis_index("lat"), lax.axis_index("lon")
+    a, home = lax.axis_index("lat"), lax.axis_index("lon")
+    chips = n_lon // 2
+    chip, core = home // 2, lax.rem(home, 2)
+    partner = home + 1 - 2 * core
+    traded = chip < chips // 2
+    b = jnp.where(traded, partner, home)
     ccols, ecols = pf.shape[1], vf.shape[1]
     rows = pf.shape[0]
     pieces = len(OFFSETS)
@@ -52,14 +58,18 @@
     side = math.isqrt(n_lat)
     slow = jnp.where(lax.rem(a, side) == side - 1, 1, -1)
     quick = -slow
-    far = 2 * lax.rem(b, 2) - 1
-    near = -far
-    sends = [
-        (slow, far), (slow, near), (slow, 0), (quick, far), (0, far),
-        (quick, near), (quick, 0), (0, near),
-    ]
-    p_batches = (range(0, 1), range(1, 5), range(5, 8),)
-    v_batches = (range(0, 1), range(1, 3), range(3, 5), range(5, 8),)
+
+    def ordered(far):
+        near = -far
+        return [
+            (slow, far), (slow, near), (slow, 0), (quick, far), (0, far),
+            (quick, near), (quick, 0), (0, near),
+        ]
+
+    home_sends = ordered(2 * core - 1)
+    sends = ordered(2 * lax.rem(b, 2) - 1)
+    p_batches = (range(0, 2), range(2, 5), range(5, 8),)
+    v_batches = (range(0, 2), range(2, 5), range(5, 8),)
 
     def if_there(p, fn):
         if isinstance(p, int) and p == 0:
@@ -67,26 +77,66 @@
         else:
             pl.when((a + p >= 0) & (a + p < n_lat))(fn)
 
-    def target(p, q):
-        return (a + p, lax.rem(b + q + n_lon, n_lon))
-
+    def around(sector, q):
+        return lax.rem(sector + q + n_lon, n_lon)
+
+    def worker(sector):
+        return jnp.where(sector < 2 * (chips // 2), sector + 1 - 2 * lax.rem(sector, 2), sector)
+
+    loads = [
+        pltpu.make_async_copy(x, y, in_sem.at[k])
+        for k, (x, y) in enumerate(((p_hbm, p_home), (sc_hbm, sc_home)))
+    ]
+    for load in loads:
+        load.start()
+
+    bands = (a + n_lat - 1) // n_lat + (2 * n_lat - 2 - a) // n_lat
     barrier = pltpu.get_barrier_semaphore()
+    across_out = around(b, 2 * lax.rem(b, 2) - 1)
+    across_home = around(home, 2 * core - 1)
+    doubled = across_out < 2 * (chips // 2)
     for lat_step in (-1, 1, 0):
         def greet(lat_step=lat_step):
-            for offset in OFFSETS:
-                if offset[0] == lat_step:
-                    pl.semaphore_signal(
-                        barrier, inc=1, device_id=target(*offset), device_id_type=MESH
-                    )
+            def signal(sector):
+                pl.semaphore_signal(
+                    barrier, inc=1, device_id=(a + lat_step, sector), device_id_type=MESH
+                )
+            signal(across_out)
+            pl.when(doubled)(lambda: signal(worker(across_out)))
+            pl.when(traded)(lambda: signal(worker(across_home)))
+            signal(partner)
+            if lat_step != 0:
+                signal(home)
         if_there(lat_step, greet)
 
-    pairs = [
-        (p_hbm, p_row), (sc_hbm, sc), (ec_hbm, ec), (v_hbm, v_row), (se_hbm, se),
-        (inv_hbm, inv_dual), (coupling_hbm, coupling), (ce_hbm, ce), (weight_hbm, weight), (sound_hbm, sound),
+    kept = [p_home, sc_home, ec_home, v_home, se_home, inv_home, coupling_home, ce_home, weight_home, sound_home]
+    held = [p_row, sc, ec, v_row, se, inv_dual, coupling, ce, weight, sound]
+    given = [p_hbm, sc_hbm, ec_hbm, v_hbm, se_hbm, inv_hbm, coupling_hbm, ce_hbm, weight_hbm, sound_hbm]
+    loads += [
+        pltpu.make_async_copy(x, y, in_sem.at[k + 2]) for k, (x, y) in enumerate(zip(given[2:], kept[2:]))
     ]
-    loads = [pltpu.make_async_copy(x, y, in_sem.at[k]) for k, (x, y) in enumerate(pairs)]
-    for load in loads:
+    fills = [pltpu.make_async_copy(x, y, work_sem.at[k]) for k, (x, y) in enumerate(zip(given, held))]
+    gifts = [
+        pltpu.make_async_remote_copy(
+            src_ref=x, dst_ref=y, send_sem=in_sem.at[k], recv_sem=work_sem.at[k],
+            device_id=(a, partner), device_id_type=MESH,
+        )
+        for k, (x, y) in enumerate(zip(kept, held))
+    ]
+    returns = [
+        pltpu.make_async_remote_copy(
+            src_ref=x, dst_ref=y, send_sem=in_sem.at[k], recv_sem=work_sem.at[k],
+            device_id=(a, partner), device_id_type=MESH,
+        )
+        for k, (x, y) in enumerate(((pf, pf_home), (vf, vf_home)))
+    ]
+    for load in loads[2:]:
         load.start()
+
+    @pl.when(jnp.logical_not(traded))
+    def _():
+        for fill in fills:
+            fill.start()
 
     def clear(p):
         def fill():
@@ -94,6 +144,7 @@
                 if offset[0] == p:
                     for turn in range(2):
                         p_halo[turn, slot] = jnp.zeros(p_halo.shape[2:], F32)
+                    for turn in range(NSUB):
                         v_halo[turn, slot] = jnp.zeros(v_halo.shape[2:], F32)
         return fill
 
@@ -103,35 +154,58 @@
     work[nlev - nlev % 8 :, :] = jnp.zeros_like(pf[nlev - nlev % 8 :, :])
     vf[...] = jnp.zeros_like(vf)
 
-    def copy(i, send, land, ss, rs, turn):
-        p, q = sends[i]
+    def copy(i, route, send, land, ss, rs, turn):
+        offsets, sector, place = route
+        p, q = offsets[i]
         member = member_of(p, q)
         return pltpu.make_async_remote_copy(
             src_ref=send.at[pl.ds(i * rows, rows)], dst_ref=land.at[turn, 7 - member],
-            send_sem=ss.at[i], recv_sem=rs.at[7 - member],
-            device_id=target(p, q), device_id_type=MESH,
+            send_sem=ss.at[0], recv_sem=rs.at[0],
+            device_id=(a + p, place(around(sector, q))), device_id_type=MESH,
         )
 
-    def launch(batch, refs, turn):
+    out_route = (home_sends, home, worker)
+    mid_route = (sends, b, worker)
+    back_route = (sends, b, lambda sector: sector)
+    local = pieces - 1
+
+    def stays(i, route, fn):
+        if i == local and route is not mid_route:
+            pl.when(jnp.logical_not(traded))(fn)
+        else:
+            if_there(sends[i][0], fn)
+
+    def launch(batch, route, refs, turn):
         for i in batch:
-            if_there(sends[i][0], lambda: copy(i, *refs, turn).start())
-
-    def arrive(group, refs, turn):
-        send, land, ss, rs = refs
-        for p, q in group:
-            slot = member_of(p, q)
-
-            def wait():
-                pltpu.make_async_remote_copy(
-                    src_ref=send.at[pl.ds(0, rows)], dst_ref=land.at[turn, slot],
-                    send_sem=ss.at[0], recv_sem=rs.at[slot],
-                    device_id=target(p, q), device_id_type=MESH,
-                ).wait_recv()
-            if_there(p, wait)
-
-    def retire(refs, turn):
-        for i in range(pieces):
-            if_there(sends[i][0], lambda: copy(i, *refs, turn).wait_send())
+            stays(i, route, lambda: copy(i, route, *refs, turn).start())
+            if i == local and route is not mid_route:
+                send, land = refs[:2]
+                slot = 7 - member_of(*route[0][i])
+
+                @pl.when(traded)
+                def _():
+                    land[turn, slot] = send[span(i), :]
+
+    def settle(route, refs, fn):
+        send, _, ss, rs = refs
+        numbers = {2 + 3 * n for n in ((1, 2) if n_lat > 2 else (n_lat - 1,))}
+        total = 2 + 3 * bands
+        if route is not mid_route:
+            numbers |= {n - 1 for n in numbers}
+            total = total - traded.astype(jnp.int32)
+        for n in sorted(numbers):
+            whole = send.at[pl.ds(0, n * rows)]
+            both = pltpu.make_async_remote_copy(
+                src_ref=whole, dst_ref=whole, send_sem=ss.at[0], recv_sem=rs.at[0],
+                device_id=(a, partner), device_id_type=MESH,
+            )
+            pl.when(total == n)(lambda: fn(both))
+
+    def arrive(route, refs):
+        settle(route, refs, lambda copies: copies.wait_recv())
+
+    def retire(route, refs):
+        settle(route, refs, lambda copies: copies.wait_send())
 
     def pick(tiles, firsts, index):
         shape = tiles[0].shape
@@ -190,15 +264,15 @@
             else:
                 grad[:, cols] = total
 
-    def add_divergence(part, fresh, last):
+    def add_divergence(part, fresh, last, sides, factors, speeds, values):
         for k in range(ccols // LANES):
             cols = slice(k * LANES, (k + 1) * LANES)
             total = None if fresh else div[:, cols]
             for j in range(3):
-                term = pick(*part, spread(ce[j, :, cols], edges, ecols)) * weight[j, :, cols]
+                term = pick(*part, spread(sides[j, :, cols], edges, ecols)) * factors[j, :, cols]
                 total = term if total is None else total + term
             if last:
-                right = pf[:, cols] - sound[:, cols] * total
+                right = values[:, cols] - speeds[:, cols] * total
                 work[0:nlev, cols] = right[0:nlev] * t_inv[:, cols]
             else:
                 div[:, cols] = total
@@ -246,7 +320,7 @@
     def across(k, batch):
         return pl.ds(k + batch.start * rows, len(batch), stride=rows)
 
-    def own_columns():
+    def own_columns(coupling):
         def put(k, inverse, low, up):
             t_inv[level(k), :] = inverse
             t_up[level(k), :] = up
@@ -287,27 +361,44 @@
             hold, lambda k: work[level(k), :], put,
         )
 
+    h_refs = (h_send, p_halo, p_ss, p_rs)
     p_refs = (p_send, p_halo, p_ss, p_rs)
     v_refs = (v_send, v_halo, v_ss, v_rs)
+    f_refs = (v_send, v_halo, v_ss, f_rs)
     for load in loads[:2]:
         load.wait()
     for k in range(nlev):
+        pf[level(k), :] = p_home[k]
+    own = own_part(tiles_of(pf, ccols))
+    for i, offset in enumerate(home_sends):
+        h_send[span(i), :] = pick(*own, sc_home[0, pl.ds(member_of(*offset), 1), :])
+    reached = 2 + doubled.astype(jnp.int32) + traded.astype(jnp.int32)
+    pl.semaphore_wait(barrier, reached + (reached + 1) * bands)
+    launch(range(pieces), out_route, h_refs, 0)
+    for load in loads[2:]:
+        load.wait()
+
+    @pl.when(traded)
+    def _():
+        for gift in gifts:
+            gift.start()
+        for gift in gifts:
+            gift.wait_recv()
+
+    @pl.when(jnp.logical_not(traded))
+    def _():
+        for fill in fills:
+            fill.wait()
+
+    for k in range(nlev):
         pf[level(k), :] = p_row[k]
+        vf[level(k), 0:edges] = v_row[k]
     for i, offset in enumerate(sends):
         sc_list[i : i + 1, :] = sc[0, pl.ds(member_of(*offset), 1), :]
+        se_list[i : i + 1, :] = se[0, pl.ds(member_of(*offset), 1), :]
     own = own_part(tiles_of(pf, ccols))
     for i in range(pieces):
         p_send[span(i), :] = pick(*own, sc_list[i : i + 1, :])
-    bands = (a + n_lat - 1) // n_lat + (2 * n_lat - 2 - a) // n_lat
-    pl.semaphore_wait(barrier, 2 + 3 * bands)
-    launch(range(pieces), p_refs, 0)
-
-    for load in loads[2:]:
-        load.wait()
-    for k in range(nlev):
-        vf[level(k), 0:edges] = v_row[k]
-    for i, offset in enumerate(sends):
-        se_list[i : i + 1, :] = se[0, pl.ds(member_of(*offset), 1), :]
     blocks = range(ecols // LANES)
     index = se_list[...]
     for r in (0, 1):
@@ -326,9 +417,11 @@
             weight_list[j] = listed([weight[j, :, cut] for cut in cuts], index)
         sound_list[...] = listed([sound[:, cut] for cut in cuts], index)
 
+    here = (ce, weight, sound, pf)
     for substep in range(NSUB):
         final = substep == NSUB - 1
         turn = substep % 2
+        route = mid_route if substep else out_route
         own = own_part(tiles_of(pf, ccols))
         for i in range(pieces):
             s_grad[span(i), :] = piece_change(i, own)
@@ -336,46 +429,69 @@
         if substep == 0:
             compose_cells()
             piece_columns()
-            own_columns()
+            own_columns(coupling)
         else:
-            retire(v_refs, 1 - turn)
-        arrive(sends, p_refs, turn)
+            retire(mid_route, v_refs)
+        arrive(route, p_refs)
         part = halo_part(p_halo, turn, sends, ccols // LANES)
         for batch in v_batches:
             for i in batch:
                 change = s_grad[span(i), :] + piece_change(i, part)
                 v_send[span(i), :] = v_send[span(i), :] - scale_list[i : i + 1, :] * change
-            launch(batch, v_refs, turn)
+            if final:
+                launch(batch, back_route, f_refs, substep)
+            else:
+                launch(batch, mid_route, v_refs, substep)
         add_gradient(part, False, True)
         if final:
+            pl.when(traded)(returns[1].start)
+            pl.when(traded)(lambda: own_columns(coupling_home))
+            pl.when(traded)(returns[0].wait_recv)
+            pl.when(traded)(returns[1].wait_recv)
+
+            @pl.when(jnp.logical_not(traded))
+            def _():
+                pf_home[...] = pf[...]
+                vf_home[...] = vf[...]
+
             for k in range(nlev):
-                v_out[k] = vf[level(k), 0:edges]
-
-        own = own_part(tiles_of(vf, ecols))
-        if not final:
+                v_out[k] = vf_home[level(k), 0:edges]
+            own = own_part(tiles_of(vf_home, ecols))
+            here = (ce_home, weight_home, sound_home, pf_home)
+        else:
+            own = own_part(tiles_of(vf, ecols))
             for i in range(pieces):
                 s_div[span(i), :] = piece_sum(i, own)
-        add_divergence(own, True, False)
-        retire(p_refs, turn)
-        arrive(sends, v_refs, turn)
-        part = halo_part(v_halo, turn, sends, ecols // LANES)
+        add_divergence(own, True, False, *here)
+        if substep in (0, NSUB - 1):
+            sent = returns if final else gifts
+            pl.when(traded)(lambda: [x.wait_send() for x in sent] and None)
+
+        retire(route, h_refs if substep == 0 else p_refs)
         if final:
+            arrive(back_route, f_refs)
+            part = halo_part(v_halo, substep, home_sends, ecols // LANES)
+
             def put(k, value):
                 p_out[k] = value
         else:
+            arrive(mid_route, v_refs)
+            part = halo_part(v_halo, substep, sends, ecols // LANES)
             for batch in p_batches:
                 for i in batch:
                     total = s_div[span(i), :] + piece_sum(i, part)
                     s_div[span(i), :] = p_send[span(i), :] - sound_list[i : i + 1, :] * total
                 solve_pieces(batch)
-                launch(batch, p_refs, 1 - turn)
+                launch(batch, mid_route, p_refs, 1 - turn)
 
             def put(k, value):
                 pf[level(k), :] = value
-        add_divergence(part, False, True)
+        add_divergence(part, False, True, *here)
         solve_own(put)
-
-    retire(v_refs, turn)
+        if substep == NSUB - 2:
+            pl.when(traded)(returns[0].start)
+
+    retire(back_route, f_refs)
 
 
 def write_out(p_ref, v_ref, p_out, v_out, sem):
@@ -401,7 +517,6 @@
     rows, ecols = round_up(nlev, 32), round_up(edges, 128)
     hbm = pl.BlockSpec(memory_space=pltpu.HBM)
     vmem = pl.BlockSpec(memory_space=pltpu.VMEM)
-    dma8 = pltpu.SemaphoreType.DMA((8,))
     args = [level_major(x) if k in (0, 1, 3, 7, 9) else x for k, x in enumerate(args)]
 
     def body(*refs):
@@ -424,14 +539,15 @@
         ),
         in_specs=[hbm] * len(args),
         out_specs=(vmem, vmem),
-        scratch_shapes=[pltpu.VMEM(x.shape, x.dtype) for x in args] + [
-            cell_shape, edge_shape, piece_shape, piece_shape, halo_shape, halo_shape,
+        scratch_shapes=[pltpu.VMEM(x.shape, x.dtype) for x in args] * 2 + [
+            cell_shape, edge_shape, cell_shape, edge_shape, piece_shape, piece_shape, piece_shape,
+            halo_shape, pltpu.VMEM((NSUB, 8, rows, halo), F32),
             level_shape, level_shape, level_shape, pltpu.VMEM((1, cells), F32), cell_shape, edge_shape, cell_shape,
             places, places, pltpu.VMEM((2, 8, halo), jnp.int32), pltpu.VMEM((3, 8, halo), jnp.int32),
             list_shape, pltpu.VMEM((3, 8, halo), F32), list_shape,
             stack_shape, stack_shape, stack_shape, list_shape, piece_shape, piece_shape,
-            dma8, dma8, dma8, dma8,
-            pltpu.SemaphoreType.DMA((len(args),)),
+            *[pltpu.SemaphoreType.DMA((1,))] * 5,
+            *[pltpu.SemaphoreType.DMA((len(args),))] * 2,
         ],
         compiler_params=pltpu.CompilerParams(
             collective_id=0, has_side_effects=True, vmem_limit_bytes=66_000_000

time: 34.6 us -> 33.2 us (0.960)
  Pallas kernels: 33.8 us -> 32.4 us
    pallas_call x1, Pallas kernels: 33.1 us -> 31.8 us  [on_device(): pl.pallas_call(body, name='substeps', out_shape=(pltpu.VMEM(args[0].shape...]
where the time goes in v2:
time: 33.2 us; the launch traced here: 33.1 us
  Pallas kernels  32.4 us (98%)
  between operations  0.64 us (2%)
    pallas_call x1, Pallas kernels, on_device(): pl.pallas_call(body, name='substeps', out_shape=(pltpu.VMEM(args[0].shape...  31.8 us
    pallas_call x1, Pallas kernels, on_device(): pl.pallas_call(write_out, name='write_out', out_shape=tuple((jax.ShapeDty...  0.69 us

profile of v2, /device:TPU:0, one launch (start us, length us, event | category | flops | bytes accessed | tf_op | source)
XLA Modules:
  0.0 33.1 jit_solution(5355833598617385639)
XLA Ops:
  0.6 31.8 %substeps.1 = (f32[30,1,640]{2,1,0:T(1,128)S(1)}, f32[30,1,960]{2,1,0:T(1,128)S(1)}) custom-call(f32[30,1,640]{2,1,0:T(1,128)} %bitcast.8, f32[30,1,960]{2,1,0:T(1,128)} %bitcast.7, s32[1,2,960]{2,1,0:T(2,128)} %refs_2_.1, s32[3,1,640]{2,1,0:T(1,128)} %bitcast.10, s32[1,8,128]{2,1,0:T(8,128)} %refs_4_.1, s32[1,8,128]{2,1,0:T(8,128)} %refs_5_.1, ...), custom_call_target="tpu_custom_call" | custom-call | tf_op jit(solution)/shard_map/substeps/pallas_call | solution.py:533
  32.4 0.7 %write_out.1 = (f32[30,1,640]{2,1,0:T(1,128)}, f32[30,1,960]{2,1,0:T(1,128)}) custom-call(f32[30,1,640]{2,1,0:T(1,128)S(1)} %get-tuple-element.6.p_ref, f32[30,1,960]{2,1,0:T(1,128)S(1)} %get-tuple-element.7.v_ref), custom_call_target="tpu_custom_call" | custom-call | tf_op jit(solution)/shard_map/write_out/pallas_call | solution.py:556

commit v3 on v2

--- a/solution.py
+++ b/solution.py
@@ -68,8 +68,8 @@
 
     home_sends = ordered(2 * core - 1)
     sends = ordered(2 * lax.rem(b, 2) - 1)
-    p_batches = (range(0, 2), range(2, 5), range(5, 8),)
-    v_batches = (range(0, 2), range(2, 5), range(5, 8),)
+    p_batches = (range(0, 2), range(2, 4), range(4, 6), range(6, 8),)
+    v_batches = (range(0, 2), range(2, 4), range(4, 6), range(6, 8),)
 
     def if_there(p, fn):
         if isinstance(p, int) and p == 0:
@@ -159,7 +159,7 @@
         p, q = offsets[i]
         member = member_of(p, q)
         return pltpu.make_async_remote_copy(
-            src_ref=send.at[pl.ds(i * rows, rows)], dst_ref=land.at[turn, 7 - member],
+            src_ref=send.at[pl.ds(i * rows, nlev)], dst_ref=land.at[turn, 7 - member, pl.ds(0, nlev)],
             send_sem=ss.at[0], recv_sem=rs.at[0],
             device_id=(a + p, place(around(sector, q))), device_id_type=MESH,
         )
@@ -194,7 +194,7 @@
             numbers |= {n - 1 for n in numbers}
             total = total - traded.astype(jnp.int32)
         for n in sorted(numbers):
-            whole = send.at[pl.ds(0, n * rows)]
+            whole = send.at[pl.ds(0, n * nlev)]
             both = pltpu.make_async_remote_copy(
                 src_ref=whole, dst_ref=whole, send_sem=ss.at[0], recv_sem=rs.at[0],
                 device_id=(a, partner), device_id_type=MESH,

time: 33.2 us -> 32.8 us (0.988)
  Pallas kernels: 32.4 us -> 32 us
    pallas_call x1, Pallas kernels: 31.8 us -> 31.3 us  [on_device(): pl.pallas_call(body, name='substeps', out_shape=(pltpu.VMEM(args[0].shape...]
where the time goes in v3:
time: 32.8 us; the launch traced here: 32.6 us
  Pallas kernels  32 us (98%)
  between operations  0.64 us (2%)
    pallas_call x1, Pallas kernels, on_device(): pl.pallas_call(body, name='substeps', out_shape=(pltpu.VMEM(args[0].shape...  31.3 us
    pallas_call x1, Pallas kernels, on_device(): pl.pallas_call(write_out, name='write_out', out_shape=tuple((jax.ShapeDty...  0.69 us

profile of v3, /device:TPU:0, one launch (start us, length us, event | category | flops | bytes accessed | tf_op | source)
XLA Modules:
  0.0 32.6 jit_solution(6211176299230698101)
XLA Ops:
  0.6 31.3 %substeps.1 = (f32[30,1,640]{2,1,0:T(1,128)S(1)}, f32[30,1,960]{2,1,0:T(1,128)S(1)}) custom-call(f32[30,1,640]{2,1,0:T(1,128)} %bitcast.8, f32[30,1,960]{2,1,0:T(1,128)} %bitcast.7, s32[1,2,960]{2,1,0:T(2,128)} %refs_2_.1, s32[3,1,640]{2,1,0:T(1,128)} %bitcast.10, s32[1,8,128]{2,1,0:T(8,128)} %refs_4_.1, s32[1,8,128]{2,1,0:T(8,128)} %refs_5_.1, ...), custom_call_target="tpu_custom_call" | custom-call | tf_op jit(solution)/shard_map/substeps/pallas_call | solution.py:533
  31.9 0.7 %write_out.1 = (f32[30,1,640]{2,1,0:T(1,128)}, f32[30,1,960]{2,1,0:T(1,128)}) custom-call(f32[30,1,640]{2,1,0:T(1,128)S(1)} %get-tuple-element.6.p_ref, f32[30,1,960]{2,1,0:T(1,128)S(1)} %get-tuple-element.7.v_ref), custom_call_target="tpu_custom_call" | custom-call | tf_op jit(solution)/shard_map/write_out/pallas_call | solution.py:556

commit v4 on v3

--- a/solution.py
+++ b/solution.py
@@ -69,7 +69,7 @@
     home_sends = ordered(2 * core - 1)
     sends = ordered(2 * lax.rem(b, 2) - 1)
     p_batches = (range(0, 2), range(2, 4), range(4, 6), range(6, 8),)
-    v_batches = (range(0, 2), range(2, 4), range(4, 6), range(6, 8),)
+    v_batches = (range(0, 1), range(1, 2), range(2, 4), range(4, 6), range(6, 8),)
 
     def if_there(p, fn):
         if isinstance(p, int) and p == 0:

time: 32.8 us -> 32.8 us (level)
  no operation moved by 1% of the time
where the time goes in v4:
time: 32.8 us; the launch traced here: 32.6 us
  Pallas kernels  32 us (98%)
  between operations  0.64 us (2%)
    pallas_call x1, Pallas kernels, on_device(): pl.pallas_call(body, name='substeps', out_shape=(pltpu.VMEM(args[0].shape...  31.3 us
    pallas_call x1, Pallas kernels, on_device(): pl.pallas_call(write_out, name='write_out', out_shape=tuple((jax.ShapeDty...  0.69 us

profile of v4, /device:TPU:0, one launch (start us, length us, event | category | flops | bytes accessed | tf_op | source)
XLA Modules:
  0.0 32.6 jit_solution(13932040929057044440)
XLA Ops:
  0.6 31.3 %substeps.1 = (f32[30,1,640]{2,1,0:T(1,128)S(1)}, f32[30,1,960]{2,1,0:T(1,128)S(1)}) custom-call(f32[30,1,640]{2,1,0:T(1,128)} %bitcast.8, f32[30,1,960]{2,1,0:T(1,128)} %bitcast.7, s32[1,2,960]{2,1,0:T(2,128)} %refs_2_.1, s32[3,1,640]{2,1,0:T(1,128)} %bitcast.10, s32[1,8,128]{2,1,0:T(8,128)} %refs_4_.1, s32[1,8,128]{2,1,0:T(8,128)} %refs_5_.1, ...), custom_call_target="tpu_custom_call" | custom-call | tf_op jit(solution)/shard_map/substeps/pallas_call | solution.py:533
  31.9 0.7 %write_out.1 = (f32[30,1,640]{2,1,0:T(1,128)}, f32[30,1,960]{2,1,0:T(1,128)}) custom-call(f32[30,1,640]{2,1,0:T(1,128)S(1)} %get-tuple-element.6.p_ref, f32[30,1,960]{2,1,0:T(1,128)S(1)} %get-tuple-element.7.v_ref), custom_call_target="tpu_custom_call" | custom-call | tf_op jit(solution)/shard_map/write_out/pallas_call | solution.py:556
